TPU v7x, 32 devices: a whole 2x2x4 slice. The times are simulated.
32 devices in a mesh: ep: 16 (over z, y, x), tp: 2 (over core).
Axes of the slice: x: 2, y: 2, z: 4, core: 2. Of those that a mesh axis runs over, the one named last changes fastest.
Arguments:
- tokens: bfloat16 [2048, 3584], P('ep', 'tp'), may hold values from -6 to 6
- routes: int32 [2048, 8], P('ep'), may hold values from 0 to 15, all different within a row; in each aligned block of 128 rows (0 to 127, 128 to 255, ...) at most 72 rows name the same one
- gate_levels: int32 [2048, 8], P('ep'), may hold values from 1 to 255
- w_gate: bfloat16 [16, 3584, 1024], P('ep', 'tp'), may hold values from -0.09375 to 0.09375
- w_up: bfloat16 [16, 3584, 1024], P('ep', 'tp'), may hold values from -0.09375 to 0.09375
- w_down: bfloat16 [16, 1024, 3584], P('ep', None, 'tp'), may hold values from -0.1875 to 0.1875
Outputs:
- mixed: bfloat16 [2048, 3584], P('ep', 'tp')
Inputs may be any that keep to these rules, and one draw needn't show every extreme that they name: `routes`: each row names 8 different experts. Among the 128 tokens of one aligned block no expert is named by more than 72 rows, and in every draw some expert is named by exactly 72 rows of some block.
All inputs are finite; a program needn't handle non-finite values.
Results may differ from a plain program's by a relative error of at most 0.0085.
Values may be sent and summed in bfloat16 or wider, within the bound.
A program may use at most 64 MiB of HBM per device.

v0:
```python
import jax
import jax.numpy as jnp
from jax import lax
from jax.sharding import PartitionSpec as P


def run_expert(inputs, gate_w, up_w, down_w):
    gate_part = jnp.dot(inputs, gate_w, preferred_element_type=jnp.float32)
    up_part = jnp.dot(inputs, up_w, preferred_element_type=jnp.float32)
    gate_sum, up_sum = (
        lax.psum_scatter(gate_part, "tp", scatter_dimension=1, tiled=True),
        lax.psum_scatter(up_part, "tp", scatter_dimension=1, tiled=True),
    )
    hidden = (jax.nn.silu(gate_sum) * up_sum).astype(jnp.bfloat16)
    output = jnp.dot(
        lax.all_gather(hidden, "tp", axis=1, tiled=True), down_w, preferred_element_type=jnp.float32
    )
    return output.astype(jnp.bfloat16)


def on_device(tokens, routes, gate_levels, w_gate, w_up, w_down):
    ep_count = lax.axis_size("ep")
    tok_rows, top_count = routes.shape
    experts_here = w_gate.shape[0]
    capacity = min(tok_rows, max(2, 9 * tok_rows * top_count // (8 * experts_here * ep_count)))
    width_local = tokens.shape[1]
    slots_each = ep_count * capacity
    slots_total = experts_here * slots_each
    flat_ids = routes.reshape(-1)
    positions = jnp.arange(tok_rows * top_count, dtype=jnp.int32)
    same_expert = flat_ids[:, None] == flat_ids[None, :]
    earlier = positions[:, None] > positions[None, :]
    slot_index = jnp.sum(same_expert & earlier, axis=1)
    destination = (
        flat_ids % experts_here * ep_count + flat_ids // experts_here
    ) * capacity + slot_index
    slot_numbers = jnp.arange(slots_total, dtype=jnp.int32)
    matches = destination.reshape(tok_rows, top_count)[:, :, None] == slot_numbers[None, None, :]
    token_slots = jnp.any(matches, axis=1).astype(jnp.bfloat16)
    outgoing = jnp.einsum(
        "ts,td->sd", token_slots, tokens, preferred_element_type=jnp.float32
    ).astype(jnp.bfloat16)
    levels = gate_levels.astype(jnp.float32)
    weights = levels / jnp.sum(levels, axis=1, keepdims=True)
    weight_high = weights.astype(jnp.bfloat16).astype(jnp.float32)
    weight_low = weights - weight_high
    table_high = jnp.sum(jnp.where(matches, weight_high[:, :, None], 0.0), axis=1).astype(
        jnp.bfloat16
    )
    table_low = jnp.sum(jnp.where(matches, weight_low[:, :, None], 0.0), axis=1).astype(
        jnp.bfloat16
    )
    arrived = lax.all_to_all(
        outgoing.reshape(experts_here, ep_count, capacity, width_local),
        "ep",
        split_axis=1,
        concat_axis=1,
        tiled=True,
    )
    expert_rows = arrived.reshape(experts_here, slots_each, width_local)
    results = [run_expert(expert_rows[0], w_gate[0], w_up[0], w_down[0])]
    produced = jnp.stack(results)
    returned = lax.all_to_all(
        produced.reshape(experts_here, ep_count, capacity, width_local),
        "ep",
        split_axis=1,
        concat_axis=1,
        tiled=True,
    )
    flat_returned = returned.reshape(slots_total, width_local)
    mixed = jnp.dot(table_high, flat_returned, preferred_element_type=jnp.float32)
    mixed = mixed + jnp.dot(table_low, flat_returned, preferred_element_type=jnp.float32)
    return mixed.astype(jnp.bfloat16)


def solution(mesh):
    in_specs = (
        P("ep", "tp"),
        P("ep", None),
        P("ep", None),
        P("ep", "tp", None),
        P("ep", "tp", None),
        P("ep", None, "tp"),
    )
    out_specs = P("ep", "tp")
    return jax.shard_map(
        on_device, mesh=mesh, in_specs=in_specs, out_specs=out_specs, check_vma=False
    )
```

profile of v0, /device:TPU:14, one launch (start us, length us, event | category | flops | bytes accessed | tf_op | source)
XLA Modules:
  0.0 286.4 jit_solution(4687454529718250434)
XLA Ops:
  6.5 0.0 copy-start
  6.5 0.0 reduce-scatter.3.cloned.1.call-start
  6.5 0.8 copy.29
  7.4 0.1 eq.30
  7.5 0.5 convert_reduce_fusion
  8.0 0.1 reduce_sum.39
  8.1 0.7 multiply_add_fusion
  8.9 0.1 copy.31
  9.0 1.5 fusion
  10.4 0.0 copy-done
  10.5 1.3 convolution_convert_fusion.1
  11.7 0.0 copy-start.3
  11.8 97.5 %all_to_all.10 = bf16[1,16,72,1792]{3,2,0,1:T(8,128)(2,1)S(1)} all-to-all(bf16[1,16,72,1792]{3,2,0,1:T(8,128)(2,1)S(1)} %bitcast.26), channel_id=1, replica_groups=mesh['ep'=16,'tp'=2] {'ep'}, dimensions={1} | all-to-all | bytes 8257536 | tf_op jit(solution)/shard_map/all_to_all | solution.py:53
  109.2 0.0 copy-start.1
  109.2 2.0 copy-done.1
  111.2 0.0 copy-done.3
  111.3 6.0 %fusion.5 = f32[1152,1024]{1,0:T(8,128)} fusion(bf16[1152,1792]{1,0:T(8,128)(2,1)S(1)} %bitcast.28, bf16[1,1792,1024]{2,1,0:T(8,128)(2,1)S(1)} %copy-done.3), kind=kOutput, calls=%fused_computation.12 | convolution fusion | flops 4227858432 | bytes 12517376 | tf_op jit(solution)/shard_map/dot_general | solution.py:8
  117.2 0.0 reduce-scatter.3.cloned.1.call-update
  117.3 0.0 reduce-scatter.5.cloned.1.call-start
  117.3 10.6 %fusion.3 = f32[1152,1024]{1,0:T(8,128)} fusion(bf16[1152,1792]{1,0:T(8,128)(2,1)} %bitcast.29, bf16[1,1792,1024]{2,1,0:T(8,128)(2,1)} %param.10), kind=kOutput, calls=%fused_computation.10 | convolution fusion | flops 4227858432 | bytes 12517376 | tf_op jit(solution)/shard_map/dot_general | solution.py:9
  127.9 0.0 reduce-scatter.5.cloned.1.call-update
  127.9 0.2 all-gather.2.cloned.1.call-start
  128.1 2.0 reduce-scatter.3.cloned.1.call-done
  130.1 16.0 %reduce-scatter.5.cloned.1.call-done = f32[1152,512]{1,0:T(8,128)} async-done(((f32[1152,1024]{1,0:T(8,128)}), f32[1152,512]{1,0:T(8,128)}) %reduce-scatter.5.cloned.1.call-update) | async-done | bytes 2359312 | tf_op jit(solution)/shard_map/reduce_scatter | solution.py:12
  146.1 4.2 %multiply_convert_fusion = bf16[1152,512]{1,0:T(8,128)(2,1)} fusion(f32[1152,512]{1,0:T(8,128)} %reduce-scatter.5.cloned.1.call-done, f32[1152,512]{1,0:T(8,128)} %reduce-scatter.3.cloned.1.call-done), kind=kLoop, calls=%fused_computation.16 | loop fusion | flops 3538944 | bytes 5898240 | tf_op jit(solution)/shard_map/convert_element_type | solution.py:14
  150.3 0.0 all-gather.2.cloned.1.call-update
  150.3 12.3 %all-gather.2.cloned.1.call-done = bf16[1152,1024]{1,0:T(8,128)(2,1)} async-done(((bf16[1152,512]{1,0:T(8,128)(2,1)}), bf16[1152,1024]{1,0:T(8,128)(2,1)}) %all-gather.2.cloned.1.call-update) | async-done | bytes 2359312 | tf_op jit(solution)/shard_map/all_gather | solution.py:16
  162.6 9.1 %convolution_convert_fusion = bf16[1152,1792]{1,0:T(8,128)(2,1)} fusion(bf16[1152,1024]{1,0:T(8,128)(2,1)} %all-gather.2.cloned.1.call-done, bf16[1,1024,1792]{2,1,0:T(8,128)(2,1)} %param.11), kind=kOutput, calls=%fused_computation | convolution fusion | flops 4229922816 | bytes 10158080 | tf_op jit(solution)/shard_map/dot_general | solution.py:15
  171.8 0.0 copy-start.2
  171.8 7.1 %all-to-all-start.1 = ((bf16[1,16,72,1792]{3,2,0,1:T(8,128)(2,1)}), bf16[1,16,72,1792]{3,2,0,1:T(8,128)(2,1)}, u32[]{:S(2)}, u32[]{:S(2)}) async-start(bf16[1,16,72,1792]{3,2,0,1:T(8,128)(2,1)} %bitcast.27), calls=%async_computation.3 | async-start | bytes 8257536 | tf_op jit(solution)/shard_map/all_to_all | solution.py:63
  178.8 0.0 copy-done.2
  178.9 0.1 copy.32
  179.0 0.1 copy.35
  179.1 3.1 %select_reduce_fusion = (bf16[128,1152]{1,0:T(8,128)(2,1)S(1)}, bf16[128,1152]{1,0:T(8,128)(2,1)S(1)}) fusion(f32[128,8]{1,0:T(8,128)S(1)} %copy.35, s32[128,8]{1,0:T(8,128)S(1)} %copy.31, f32[128,8]{1,0:T(8,128)S(1)} %copy.32), kind=kLoop, calls=%fused_computation.2 | loop fusion | flops 5603328 | bytes 602112 | tf_op jit(solution)/shard_map/reduce_sum | solution.py:50
  182.2 91.0 %all-to-all-done.1 = bf16[1,16,72,1792]{3,2,0,1:T(8,128)(2,1)} async-done(((bf16[1,16,72,1792]{3,2,0,1:T(8,128)(2,1)}), bf16[1,16,72,1792]{3,2,0,1:T(8,128)(2,1)}, u32[]{:S(2)}, u32[]{:S(2)}) %all-to-all-start.1) | async-done | bytes 4128800 | tf_op jit(solution)/shard_map/all_to_all | solution.py:63
  273.2 2.9 %fusion.12 = f32[128,1792]{1,0:T(8,128)S(1)} fusion(bf16[128,1152]{1,0:T(8,128)(2,1)S(1)} %get-tuple-element.6, bf16[1152,1792]{1,0:T(8,128)(2,1)} %bitcast.8), kind=kOutput, calls=%fused_computation.25 | convolution fusion | flops 528482304 | bytes 5341184 | tf_op jit(solution)/shard_map/dot_general | solution.py:71
  276.2 3.7 %fusion.7 = bf16[128,1792]{1,0:T(8,128)(2,1)} fusion(f32[128,1792]{1,0:T(8,128)S(1)} %fusion.12, bf16[1152,1792]{1,0:T(8,128)(2,1)} %bitcast.8, bf16[128,1152]{1,0:T(8,128)(2,1)S(1)} %get-tuple-element.5), kind=kOutput, calls=%fused_computation.15 | convolution fusion | flops 528941056 | bytes 5799936 | tf_op jit(solution)/shard_map/dot_general | solution.py:72
  (3 shorter events, 0.1 us)
Async XLA Ops:
  6.5 3.9 %copy-start = (bf16[128,1792]{1,0:T(8,128)(2,1)S(1)}, bf16[128,1792]{1,0:T(8,128)(2,1)}, u32[]{:S(2)}) copy-start(bf16[128,1792]{1,0:T(8,128)(2,1)} %param.6) | copy-start | bytes 1376260
  6.5 123.6 %reduce-scatter.3.cloned.1.call-start = ((), (), s32[]{:S(2)}) async-start(), calls=%async_computation.4 | async-start | bytes 7077888 | tf_op jit(solution)/shard_map/reduce_scatter | solution.py:11
  11.7 99.5 %copy-start.3 = (bf16[1,1792,1024]{2,1,0:T(8,128)(2,1)S(1)}, bf16[1,1792,1024]{2,1,0:T(8,128)(2,1)}, u32[]{:S(2)}) copy-start(bf16[1,1792,1024]{2,1,0:T(8,128)(2,1)} %param.9) | copy-start | bytes 11010052
  109.2 2.0 copy-start.1
  117.3 28.9 %reduce-scatter.5.cloned.1.call-start = ((), (), s32[]{:S(2)}) async-start(), calls=%async_computation.5 | async-start | bytes 7077888 | tf_op jit(solution)/shard_map/reduce_scatter | solution.py:12
  127.9 34.7 %all-gather.2.cloned.1.call-start = ((), (), s32[]{:S(2)}) async-start(), calls=%async_computation.6 | async-start | bytes 3538944 | tf_op jit(solution)/shard_map/all_gather | solution.py:16
  171.8 7.1 %copy-start.2 = (s32[128,8]{0,1:T(8,128)S(1)}, s32[128,8]{0,1:T(8,128)}, u32[]{:S(2)}) copy-start(s32[128,8]{0,1:T(8,128)} %param.8) | copy-start | bytes 12292
  171.8 101.4 %all-to-all-start.1 = ((bf16[1,16,72,1792]{3,2,0,1:T(8,128)(2,1)}), bf16[1,16,72,1792]{3,2,0,1:T(8,128)(2,1)}, u32[]{:S(2)}, u32[]{:S(2)}) async-start(bf16[1,16,72,1792]{3,2,0,1:T(8,128)(2,1)} %bitcast.27), calls=%async_computation.3 | async-start | bytes 8257536 | tf_op jit(solution)/shard_map/all_to_all | solution.py:63
Sparse Core Ops, SparseCore 0:
  117.4 12.7 reduce-scatter.2
  132.4 13.6 reduce-scatter.4
  150.5 12.1 all-gather.1
where the time goes:
time: 287 us; the launch traced here: 286 us
  waiting for transfers between devices  121 us (42%)
  blocking collectives  97.5 us (34%)
  matrix products  33.6 us (12%)
  between operations  13.2 us (5%)
  other arithmetic  9.99 us (3%)
  starting transfers between devices  7.35 us (3%)
  local copies, waits for them, and re-layouts  3.42 us (1%)
    all_to_all x1, blocking collectives, on_device(): lax.all_to_all(outgoing.reshape(experts_here, ep_count, capacity, width_l...  97.5 us
    all_to_all x1, waiting for transfers between devices, on_device(): lax.all_to_all(produced.reshape(experts_here, ep_count, capacity, width_l...  91 us
    reduce_scatter x1, waiting for transfers between devices, run_expert(): lax.psum_scatter(up_part, 'tp', scatter_dimension=1, tiled=True)  16 us
    all_gather x1, waiting for transfers between devices, run_expert(): lax.all_gather(hidden, 'tp', axis=1, tiled=True)  12.3 us
    dot_general x1, matrix products, run_expert(): up_part = jnp.dot(inputs, up_w, preferred_element_type=jnp.float32)  10.6 us
    dot_general x1, matrix products, run_expert(): jnp.dot(lax.all_gather(hidden, 'tp', axis=1, tiled=True), down_w, preferr...  9.13 us
    all_to_all x1, starting transfers between devices, on_device(): lax.all_to_all(produced.reshape(experts_here, ep_count, capacity, width_l...  7.09 us
    dot_general x1, matrix products, run_expert(): gate_part = jnp.dot(inputs, gate_w, preferred_element_type=jnp.float32)  5.98 us
  transfers between devices with their start and end apart: 4, of which 4 were waited for; matrix products, arithmetic and copies ran while one was open for 5% of the time, Pallas kernels for 0%

commit v1 on v0

--- a/solution.py
+++ b/solution.py
@@ -60,13 +60,10 @@
     expert_rows = arrived.reshape(experts_here, slots_each, width_local)
     results = [run_expert(expert_rows[0], w_gate[0], w_up[0], w_down[0])]
     produced = jnp.stack(results)
-    returned = lax.all_to_all(
-        produced.reshape(experts_here, ep_count, capacity, width_local),
-        "ep",
-        split_axis=1,
-        concat_axis=1,
-        tiled=True,
-    )
+    own = produced.reshape(experts_here, ep_count, capacity, width_local)
+    cells = jnp.split(own, lax.axis_size("ep"), axis=1)
+    received = lax.all_to_all(jnp.stack(cells), "ep", 0, 0)
+    returned = jnp.concatenate(received, axis=1)
     flat_returned = returned.reshape(slots_total, width_local)
     mixed = jnp.dot(table_high, flat_returned, preferred_element_type=jnp.float32)
     mixed = mixed + jnp.dot(table_low, flat_returned, preferred_element_type=jnp.float32)

time: 287 us -> 296 us (1.031)
  local copies, waits for them, and re-layouts: 3.42 us -> 14.9 us
    unnamed x9 -> x24, local copies, waits for them, and re-layouts: 2.89 us -> 13.7 us
where the time goes in v1:
time: 296 us
  waiting for transfers between devices  121 us (41%)
  blocking collectives  97.5 us (33%)
  matrix products  31.7 us (11%)
  local copies, waits for them, and re-layouts  14.9 us (5%)
  between operations  13.2 us (4%)
  other arithmetic  9.99 us (3%)
  starting transfers between devices  7.35 us (2%)
    all_to_all x1, blocking collectives, on_device(): lax.all_to_all(outgoing.reshape(experts_here, ep_count, capacity, width_l...  97.5 us
    all_to_all x1, waiting for transfers between devices, on_device(): received = lax.all_to_all(jnp.stack(cells), 'ep', 0, 0)  91 us
    reduce_scatter x1, waiting for transfers between devices, run_expert(): lax.psum_scatter(up_part, 'tp', scatter_dimension=1, tiled=True)  16 us
    unnamed x24, local copies, waits for them, and re-layouts  13.7 us
    all_gather x1, waiting for transfers between devices, run_expert(): lax.all_gather(hidden, 'tp', axis=1, tiled=True)  12.3 us
    dot_general x1, matrix products, run_expert(): up_part = jnp.dot(inputs, up_w, preferred_element_type=jnp.float32)  10.6 us
    dot_general x1, matrix products, run_expert(): jnp.dot(lax.all_gather(hidden, 'tp', axis=1, tiled=True), down_w, preferr...  7.2 us
    all_to_all x1, starting transfers between devices, on_device(): received = lax.all_to_all(jnp.stack(cells), 'ep', 0, 0)  7.09 us
  transfers between devices with their start and end apart: 4, of which 4 were waited for; matrix products, arithmetic and copies ran while one was open for 5% of the time, Pallas kernels for 0%

profile of v1, /device:TPU:14, one launch (start us, length us, event | category | flops | bytes accessed | tf_op | source)
XLA Modules:
  0.0 296.0 jit_solution(7388869008389958239)
XLA Ops:
  6.5 0.0 copy-start
  6.5 0.0 reduce-scatter.3.cloned.1.call-start
  6.5 0.8 copy.27
  7.4 0.1 eq.30
  7.5 0.5 convert_reduce_fusion
  8.0 0.1 reduce_sum.39
  8.1 0.7 multiply_add_fusion
  8.9 0.1 copy.29
  9.0 1.5 fusion
  10.4 0.0 copy-done
  10.5 1.3 convolution_convert_fusion.1
  11.7 0.0 copy-start.3
  11.8 97.5 %all_to_all.10 = bf16[1,16,72,1792]{3,2,0,1:T(8,128)(2,1)S(1)} all-to-all(bf16[1,16,72,1792]{3,2,0,1:T(8,128)(2,1)S(1)} %bitcast.88), channel_id=1, replica_groups=mesh['ep'=16,'tp'=2] {'ep'}, dimensions={1} | all-to-all | bytes 8257536 | tf_op jit(solution)/shard_map/all_to_all | solution.py:53
  109.2 0.0 copy-start.1
  109.2 2.0 copy-done.1
  111.2 0.0 copy-done.3
  111.3 6.0 %fusion.5 = f32[1152,1024]{1,0:T(8,128)} fusion(bf16[1152,1792]{1,0:T(8,128)(2,1)S(1)} %bitcast.105, bf16[1,1792,1024]{2,1,0:T(8,128)(2,1)S(1)} %copy-done.3), kind=kOutput, calls=%fused_computation.12 | convolution fusion | flops 4227858432 | bytes 12517376 | tf_op jit(solution)/shard_map/dot_general | solution.py:8
  117.2 0.0 reduce-scatter.3.cloned.1.call-update
  117.3 0.0 reduce-scatter.5.cloned.1.call-start
  117.3 10.6 %fusion.3 = f32[1152,1024]{1,0:T(8,128)} fusion(bf16[1152,1792]{1,0:T(8,128)(2,1)} %bitcast.106, bf16[1,1792,1024]{2,1,0:T(8,128)(2,1)} %param.10), kind=kOutput, calls=%fused_computation.10 | convolution fusion | flops 4227858432 | bytes 12517376 | tf_op jit(solution)/shard_map/dot_general | solution.py:9
  127.9 0.0 reduce-scatter.5.cloned.1.call-update
  127.9 0.2 all-gather.2.cloned.1.call-start
  128.1 2.0 reduce-scatter.3.cloned.1.call-done
  130.1 16.0 %reduce-scatter.5.cloned.1.call-done = f32[1152,512]{1,0:T(8,128)} async-done(((f32[1152,1024]{1,0:T(8,128)}), f32[1152,512]{1,0:T(8,128)}) %reduce-scatter.5.cloned.1.call-update) | async-done | bytes 2359312 | tf_op jit(solution)/shard_map/reduce_scatter | solution.py:12
  146.1 4.2 %multiply_convert_fusion = bf16[1152,512]{1,0:T(8,128)(2,1)} fusion(f32[1152,512]{1,0:T(8,128)} %reduce-scatter.5.cloned.1.call-done, f32[1152,512]{1,0:T(8,128)} %reduce-scatter.3.cloned.1.call-done), kind=kLoop, calls=%fused_computation.16 | loop fusion | flops 3538944 | bytes 5898240 | tf_op jit(solution)/shard_map/convert_element_type | solution.py:14
  150.3 0.0 all-gather.2.cloned.1.call-update
  150.3 12.3 %all-gather.2.cloned.1.call-done = bf16[1152,1024]{1,0:T(8,128)(2,1)} async-done(((bf16[1152,512]{1,0:T(8,128)(2,1)}), bf16[1152,1024]{1,0:T(8,128)(2,1)}) %all-gather.2.cloned.1.call-update) | async-done | bytes 2359312 | tf_op jit(solution)/shard_map/all_gather | solution.py:16
  162.6 7.2 %convolution_convert_fusion = bf16[1152,1792]{1,0:T(8,128)(2,1)S(1)} fusion(bf16[1152,1024]{1,0:T(8,128)(2,1)} %all-gather.2.cloned.1.call-done, bf16[1,1024,1792]{2,1,0:T(8,128)(2,1)} %param.11), kind=kOutput, calls=%fused_computation | convolution fusion | flops 4229922816 | bytes 10158080 | tf_op jit(solution)/shard_map/dot_general | solution.py:15
  169.8 0.7 fusion.26
  170.5 0.7 fusion.25
  171.3 0.7 fusion.24
  172.0 0.7 fusion.23
  172.7 0.7 fusion.22
  173.4 0.7 fusion.21
  174.2 0.7 fusion.20
  174.9 0.7 fusion.19
  175.6 0.7 fusion.18
  176.3 0.7 fusion.17
  177.0 0.7 fusion.16
  177.8 0.7 fusion.15
  178.5 0.7 fusion.14
  179.2 0.7 fusion.13
  179.9 0.7 fusion.12
  180.6 0.7 fusion.11
  181.3 0.0 copy-start.2
  181.3 7.1 %all-to-all-start.1 = ((bf16[16,1,1,72,1792]{4,3,2,1,0:T(8,128)(2,1)}), bf16[16,1,1,72,1792]{4,3,2,1,0:T(8,128)(2,1)}, u32[]{:S(2)}, u32[]{:S(2)}) async-start(bf16[16,1,1,72,1792]{4,3,2,1,0:T(8,128)(2,1)} %fusion.11), calls=%async_computation.3 | async-start | bytes 8257536 | tf_op jit(solution)/shard_map/all_to_all | solution.py:65
  188.4 0.0 copy-done.2
  188.5 0.1 copy.30
  188.6 0.1 copy.32
  188.7 3.1 %select_reduce_fusion = (bf16[128,1152]{1,0:T(8,128)(2,1)S(1)}, bf16[128,1152]{1,0:T(8,128)(2,1)S(1)}) fusion(f32[128,8]{1,0:T(8,128)S(1)} %copy.32, s32[128,8]{1,0:T(8,128)S(1)} %copy.29, f32[128,8]{1,0:T(8,128)S(1)} %copy.30), kind=kLoop, calls=%fused_computation.2 | loop fusion | flops 5603328 | bytes 602112 | tf_op jit(solution)/shard_map/reduce_sum | solution.py:50
  191.8 91.0 %all-to-all-done.1 = bf16[16,1,1,72,1792]{4,3,2,1,0:T(8,128)(2,1)} async-done(((bf16[16,1,1,72,1792]{4,3,2,1,0:T(8,128)(2,1)}), bf16[16,1,1,72,1792]{4,3,2,1,0:T(8,128)(2,1)}, u32[]{:S(2)}, u32[]{:S(2)}) %all-to-all-start.1) | async-done | bytes 4128800 | tf_op jit(solution)/shard_map/all_to_all | solution.py:65
  282.8 2.9 fusion.28
  285.7 3.7 %fusion.7 = bf16[128,1792]{1,0:T(8,128)(2,1)} fusion(f32[128,1792]{1,0:T(8,128)S(1)} %fusion.28, bf16[1152,1792]{1,0:T(8,128)(2,1)} %bitcast.23, bf16[128,1152]{1,0:T(8,128)(2,1)S(1)} %get-tuple-element.5), kind=kOutput, calls=%fused_computation.15 | convolution fusion | flops 528941056 | bytes 5799936 | tf_op jit(solution)/shard_map/dot_general | solution.py:69
  (3 shorter events, 0.1 us)
Async XLA Ops:
  6.5 3.9 %copy-start = (bf16[128,1792]{1,0:T(8,128)(2,1)S(1)}, bf16[128,1792]{1,0:T(8,128)(2,1)}, u32[]{:S(2)}) copy-start(bf16[128,1792]{1,0:T(8,128)(2,1)} %param.6) | copy-start | bytes 1376260
  6.5 123.6 %reduce-scatter.3.cloned.1.call-start = ((), (), s32[]{:S(2)}) async-start(), calls=%async_computation.4 | async-start | bytes 7077888 | tf_op jit(solution)/shard_map/reduce_scatter | solution.py:11
  11.7 99.5 %copy-start.3 = (bf16[1,1792,1024]{2,1,0:T(8,128)(2,1)S(1)}, bf16[1,1792,1024]{2,1,0:T(8,128)(2,1)}, u32[]{:S(2)}) copy-start(bf16[1,1792,1024]{2,1,0:T(8,128)(2,1)} %param.9) | copy-start | bytes 11010052
  109.2 2.0 copy-start.1
  117.3 28.9 %reduce-scatter.5.cloned.1.call-start = ((), (), s32[]{:S(2)}) async-start(), calls=%async_computation.5 | async-start | bytes 7077888 | tf_op jit(solution)/shard_map/reduce_scatter | solution.py:12
  127.9 34.7 %all-gather.2.cloned.1.call-start = ((), (), s32[]{:S(2)}) async-start(), calls=%async_computation.6 | async-start | bytes 3538944 | tf_op jit(solution)/shard_map/all_gather | solution.py:16
  181.3 7.1 %copy-start.2 = (s32[128,8]{0,1:T(8,128)S(1)}, s32[128,8]{0,1:T(8,128)}, u32[]{:S(2)}) copy-start(s32[128,8]{0,1:T(8,128)} %param.8) | copy-start | bytes 12292
  181.3 101.4 %all-to-all-start.1 = ((bf16[16,1,1,72,1792]{4,3,2,1,0:T(8,128)(2,1)}), bf16[16,1,1,72,1792]{4,3,2,1,0:T(8,128)(2,1)}, u32[]{:S(2)}, u32[]{:S(2)}) async-start(bf16[16,1,1,72,1792]{4,3,2,1,0:T(8,128)(2,1)} %fusion.11), calls=%async_computation.3 | async-start | bytes 8257536 | tf_op jit(solution)/shard_map/all_to_all | solution.py:65
Sparse Core Ops, SparseCore 0:
  117.4 12.7 reduce-scatter.2
  132.4 13.6 reduce-scatter.4
  150.5 12.1 all-gather.1
